TPU v7x, 32 devices: a whole 2x2x4 slice. The times are simulated.
32 devices in a mesh: grp: 4 (over x, core), seq: 8 (over z, y).
Axes of the slice: x: 2, y: 2, z: 4, core: 2. Of those that a mesh axis runs over, the one named last changes fastest.
Arguments:
- patches: bfloat16 [2048, 1280], P(('grp', 'seq')), may hold values from -60 to 60
- piece_ids: int32 [32, 64], P(('grp', 'seq')), may hold values from 0 to 2, never falling along the last dimension, each value on 1 to 48 neighbouring positions
- vit_gain: float32 [1280], replicated, may hold values from 0.25 to 1.75
- vit_qkv: bfloat16 [1280, 3840], replicated
- vit_out: bfloat16 [1280, 1280], replicated, may hold values from -0.15625 to 0.15625
- merge_gain: float32 [1280], replicated, may hold values from 0.25 to 1.75
- merge_up: bfloat16 [5120, 5120], P(None, 'seq'), may hold values from -0.078125 to 0.078125
- merge_down: bfloat16 [5120, 8192], P(None, 'seq'), may hold values from -0.078125 to 0.078125
- dest: int32 [512], P(('grp', 'seq')), may hold values from 0 to 7, as said below
- tokens: bfloat16 [8192, 8192], P(('grp', 'seq')), may hold values from -60 to 60
- image_index: int32 [8192], P(('grp', 'seq')), may hold values from 0 to 32, as said below
- doc_lengths: int32 [4, 4], P('grp'), may hold values from 1 to 1024, 2048 in all within a row
- attn_gain: float32 [8192], replicated, may hold values from 0.25 to 1.75
- attn_qkv: bfloat16 [8192, 768], P(('grp', 'seq'))
- attn_out: bfloat16 [512, 8192], P(None, ('grp', 'seq')), may hold values from -0.25 to 0.25
Outputs:
- layer_out: bfloat16 [8192, 8192], P(('grp', 'seq'))
Inputs may be any that keep to these rules, and one draw needn't show every extreme that they name: `dest`: within each aligned block of 16 rows (one device's merged rows), exactly 4 distinct values occur, each exactly 4 times, and in every group one device is named by every device of the group. `image_index`: 32 marks a text token. A value k < 32 on a device names the merged row that the device of seq index k // 4 in its group sends to it as its (k % 4)-th row in row order; each such row is named by exactly one token of the receiving device, and no other values occur. `piece_ids`: piece numbers never fall within a window. `doc_lengths`: each group's documents fill its 2048 positions.
All inputs are finite; a program needn't handle non-finite values.
Results may differ from a plain program's by a relative error of at most 0.0093.
The roundings to bfloat16 on the way count: a program that leaves them out, or rounds other values in their place, can miss the bound.
Values may be sent and summed in bfloat16 or wider, within the bound.
A program may use at most 192 MiB of HBM per device.

v0:
```python
import jax
import jax.numpy as jnp
from jax import lax
from jax.sharding import PartitionSpec as P

VHEADS = 16
WIN = 64


EPSILON = 1e-06


def from_behind(value, axis, steps):
    count = lax.axis_size(axis)
    first, last = (max(0, -steps), min(count, count - steps))
    return lax.ppermute(value, axis, [(source, source + steps) for source in range(first, last)])


def rms_scale(inputs, gain):
    mean_square = jnp.mean(inputs * inputs, axis=-1, keepdims=True)
    return inputs * lax.rsqrt(mean_square + EPSILON) * gain


def softmax_mix(scores, allowed, value_collection, spec):
    scores = jnp.where(allowed[None], scores, -1e30)
    highest = jnp.max(scores, axis=-1, keepdims=True)
    weights = jnp.exp(scores - highest)
    totals = jnp.sum(weights, axis=-1)
    mixture = jnp.einsum(
        spec, weights.astype(jnp.bfloat16), value_collection, preferred_element_type=jnp.float32
    )
    return mixture / jnp.transpose(totals)[:, :, None]


def window_layer(patch_rows, piece_rows, vit_gain, vit_qkv, vit_out, merge_gain):
    row_count, features = patch_rows.shape
    head_dim = features // VHEADS
    residual = patch_rows.astype(jnp.float32)
    normed = rms_scale(residual, vit_gain).astype(jnp.bfloat16)
    projected = jnp.dot(normed, vit_qkv, preferred_element_type=jnp.float32).astype(jnp.bfloat16)
    queries = projected[:, :features].reshape(row_count, VHEADS, head_dim)
    key_set = projected[:, features : 2 * features].reshape(row_count, VHEADS, head_dim)
    value_collection = projected[:, 2 * features :].reshape(row_count, VHEADS, head_dim)
    scores = jnp.einsum(
        "qhd,khd->hqk", queries, key_set, preferred_element_type=jnp.float32
    ) * head_dim ** (-0.5)
    frames = jnp.arange(row_count, dtype=jnp.int32) // WIN
    allowed = (frames[:, None] == frames[None, :]) & (piece_rows[:, None] == piece_rows[None, :])
    mixture = softmax_mix(scores, allowed, value_collection, "hqk,khd->qhd")
    mixture = mixture.reshape(row_count, features).astype(jnp.bfloat16)
    residual = residual + jnp.dot(mixture, vit_out, preferred_element_type=jnp.float32)
    merge_input = rms_scale(residual, merge_gain).astype(jnp.bfloat16)
    return merge_input.reshape(row_count // 4, 4 * features)


def attend(query_rows, query_pos, query_start, key_value, key_pos):
    row_count = query_rows.shape[0]
    head_dim = key_value.shape[1] // 2
    heads = query_rows.shape[1] // head_dim
    queries = query_rows.reshape(row_count, heads, head_dim)
    scores = jnp.einsum(
        "qhd,kd->hqk", queries, key_value[:, :head_dim], preferred_element_type=jnp.float32
    ) * head_dim ** (-0.5)
    allowed = (key_pos[None, :] >= query_start[:, None]) & (key_pos[None, :] <= query_pos[:, None])
    mixture = softmax_mix(scores, allowed, key_value[:, head_dim:], "hqk,kd->qhd")
    return mixture.reshape(row_count, heads * head_dim).astype(jnp.bfloat16)


def slot_numbers(targets):
    row_count = targets.shape[-1]
    order = jnp.arange(row_count, dtype=jnp.int32)
    same = targets[..., :, None] == targets[..., None, :]
    earlier = order[None, :] < order[:, None]
    return jnp.sum(same & earlier, axis=-1)


def on_device(
    patches,
    piece_ids,
    vit_gain,
    vit_qkv,
    vit_out,
    merge_gain,
    merge_up,
    merge_down,
    dest,
    tokens,
    image_index,
    doc_lengths,
    attn_gain,
    attn_qkv,
    attn_out,
):
    features = patches.shape[1]
    block_len = WIN
    patch_blocks = patches.reshape(-1, block_len, features)
    merge_input = lax.map(
        lambda parts: window_layer(parts[0], parts[1], vit_gain, vit_qkv, vit_out, merge_gain),
        (patch_blocks, piece_ids),
    ).reshape(-1, 4 * features)
    own_rows = merge_input.shape[0]
    seq_count = lax.axis_size("seq")
    seq_index = lax.axis_index("seq")
    hidden_part = jax.nn.gelu(
        jnp.dot(
            lax.all_gather(merge_input, "seq", axis=0, tiled=True),
            merge_up,
            preferred_element_type=jnp.float32,
        ),
        approximate=False,
    ).astype(jnp.bfloat16)
    column_part = jnp.dot(
        lax.all_gather(hidden_part, "seq", axis=1, tiled=True),
        merge_down,
        preferred_element_type=jnp.float32,
    ).astype(jnp.bfloat16)
    capacity = own_rows // (seq_count // 2)
    slots = seq_count * capacity
    receivers = jnp.arange(seq_count, dtype=jnp.int32)
    slot_ids = jnp.arange(capacity, dtype=jnp.int32)
    home_rows = lax.all_to_all(column_part, "seq", split_axis=0, concat_axis=1, tiled=True)
    order = slot_numbers(dest)
    select = (dest[None, None, :] == receivers[:, None, None]) & (
        order[None, None, :] == slot_ids[None, :, None]
    )
    outgoing = jnp.einsum(
        "dcj,jf->dcf", select.astype(jnp.bfloat16), home_rows, preferred_element_type=jnp.float32
    ).astype(jnp.bfloat16)
    arrived = lax.all_to_all(outgoing, "seq", split_axis=0, concat_axis=0, tiled=True).reshape(
        slots, -1
    )
    slot_all = jnp.arange(slots, dtype=jnp.int32)
    picker = (image_index[:, None] == slot_all[None, :]).astype(jnp.bfloat16)
    pictured = jnp.dot(picker, arrived, preferred_element_type=jnp.float32).astype(jnp.bfloat16)
    layer_in = jnp.where((image_index < slots)[:, None], pictured, tokens)
    tok_rows = tokens.shape[0]
    normed = rms_scale(layer_in.astype(jnp.float32), attn_gain).astype(jnp.bfloat16)
    projected = jnp.dot(
        normed,
        lax.all_gather(attn_qkv, ("grp", "seq"), axis=0, tiled=True),
        preferred_element_type=jnp.float32,
    ).astype(jnp.bfloat16)
    query_width = attn_out.shape[0]
    queries = projected[:, :query_width]
    key_value = projected[:, query_width:]
    head_dim = key_value.shape[1] // 2
    head_count = query_width // head_dim
    positions = seq_index * tok_rows + jnp.arange(tok_rows, dtype=jnp.int32)
    lengths = doc_lengths[0]
    starts = jnp.cumsum(lengths) - lengths
    doc_start = jnp.max(
        jnp.where(starts[None, :] <= positions[:, None], starts[None, :], 0), axis=1
    )
    reach = seq_count // 2
    buffer = jnp.zeros(((reach + 1) * tok_rows, key_value.shape[1]), key_value.dtype)
    buffer = lax.dynamic_update_slice_in_dim(buffer, key_value, reach * tok_rows, 0)

    def step_back(turn, state):
        current, filled = state
        current = from_behind(current, "seq", 1)
        filled = lax.dynamic_update_slice_in_dim(filled, current, (reach - turn) * tok_rows, 0)
        return (current, filled)

    key_rows = lax.fori_loop(1, reach + 1, step_back, (key_value, buffer))[1]
    key_pos = (seq_index - reach) * tok_rows + jnp.arange(key_rows.shape[0], dtype=jnp.int32)
    block_rows = min(tok_rows, 512)
    head_queries = queries.reshape(tok_rows, head_count, head_dim).transpose(1, 0, 2)

    def one_head(head_rows):
        return lax.map(
            lambda parts: attend(parts[0], parts[1], parts[2], key_rows, key_pos),
            (
                head_rows.reshape(-1, block_rows, head_dim),
                positions.reshape(-1, block_rows),
                doc_start.reshape(-1, block_rows),
            ),
        ).reshape(tok_rows, head_dim)

    attended = lax.map(one_head, head_queries).transpose(1, 0, 2).reshape(tok_rows, query_width)
    update = jnp.dot(
        attended,
        lax.all_gather(attn_out, ("grp", "seq"), axis=1, tiled=True),
        preferred_element_type=jnp.float32,
    )
    return (layer_in.astype(jnp.float32) + update).astype(jnp.bfloat16)


def solution(mesh):
    placed = (
        P(("grp", "seq"), None),
        P(("grp", "seq"), None),
        P(),
        P(),
        P(),
        P(),
        P(None, "seq"),
        P(None, "seq"),
        P(("grp", "seq")),
        P(("grp", "seq"), None),
        P(("grp", "seq")),
        P("grp", None),
        P(),
        P(("grp", "seq"), None),
        P(None, ("grp", "seq")),
    )
    return jax.shard_map(
        on_device, mesh=mesh, in_specs=placed, out_specs=P(("grp", "seq"), None), check_vma=False
    )
```

profile of v0, /device:TPU:0, one launch (start us, length us, event | category | flops | bytes accessed | tf_op | source)
XLA Modules:
  0.0 336.6 jit_solution(14184736836307715326)
XLA Ops:
  6.5 1.2 fusion.36
  7.8 5.8 %convolution_convert_fusion.2 = bf16[64,3840]{1,0:T(8,128)(2,1)S(1)} fusion(bf16[1280,3840]{1,0:T(8,128)(2,1)} %param.22, bf16[64,1280]{1,0:T(8,128)(2,1)} %param.19, f32[1280]{0:T(1024)} %param.21, f32[64]{0:T(128)S(1)} %add_rsqrt_fusion.2), kind=kOutput, calls=%fused_computation.33 | convolution fusion | flops 629719040 | bytes 10491136 | tf_op jit(solution)/shard_map/while/body/eval_jaxpr/dot_general | solution.py:40
  13.6 0.8 fusion.63
  14.4 2.0 reshape.346
  16.4 2.0 reshape.347
  18.4 2.0 reshape.345
  20.4 0.1 compare_and_fusion
  20.5 1.3 fusion.64
  21.8 0.1 fusion.34
  21.9 1.3 fusion.33
  23.2 0.9 copy.44
  24.1 1.9 convert_element_type.84
  26.0 1.7 multiply_reduce_fusion
  27.7 0.1 multiply_convert_fusion
  27.8 0.8 reshape.348
  28.7 44.6 %all-gather.5.cloned.1.call-done = bf16[128,5120]{1,0:T(8,128)(2,1)} async-done(((bf16[16,5120]{1,0:T(8,128)(2,1)}), bf16[128,5120]{1,0:T(8,128)(2,1)}) %all-gather.5.cloned.1.call-update) | async-done | bytes 1310736 | tf_op jit(solution)/shard_map/all_gather | solution.py:106
  73.3 5.8 %fusion.41 = bf16[128,640]{1,0:T(8,128)(2,1)} fusion(bf16[128,5120]{1,0:T(8,128)(2,1)} %all-gather.5.cloned.1.call-done, bf16[5120,640]{1,0:T(8,128)(2,1)} %param.25), kind=kOutput, calls=%fused_computation.56 | convolution fusion | flops 844185600 | bytes 8028160 | tf_op jit(solution)/shard_map/dot_general | solution.py:105
  79.2 0.7 all-gather.9.cloned.1.call-update
  79.9 0.5 all-gather.11.cloned.1.call-update
  80.4 40.2 %all-gather.7.cloned.1.call-done = bf16[128,5120]{1,0:T(8,128)(2,1)} async-done(((bf16[128,640]{1,0:T(8,128)(2,1)}), bf16[128,5120]{1,0:T(8,128)(2,1)}) %all-gather.7.cloned.1.call-update) | async-done | bytes 1310736 | tf_op jit(solution)/shard_map/all_gather | solution.py:113
  120.6 6.6 %convolution_convert_fusion.3 = bf16[128,1024]{1,0:T(8,128)(2,1)} fusion(bf16[128,5120]{1,0:T(8,128)(2,1)} %all-gather.7.cloned.1.call-done, bf16[5120,1024]{1,0:T(8,128)(2,1)} %param.26), kind=kOutput, calls=%fused_computation.44 | convolution fusion | flops 1342308352 | bytes 12058624 | tf_op jit(solution)/shard_map/dot_general | solution.py:112
  127.3 3.5 %all-to-all-start = ((bf16[8,16,1024]{2,1,0:T(8,128)(2,1)}), bf16[8,16,1024]{2,1,0:T(8,128)(2,1)S(1)}, u32[]{:S(2)}, u32[]{:S(2)}) async-start(bf16[8,16,1024]{2,1,0:T(8,128)(2,1)} %bitcast.3), calls=%async_computation | async-start | bytes 524288 | tf_op jit(solution)/shard_map/all_to_all | solution.py:121
  130.8 0.2 convert_reduce_fusion
  131.0 13.7 %all-to-all-done = bf16[8,16,1024]{2,1,0:T(8,128)(2,1)S(1)} async-done(((bf16[8,16,1024]{2,1,0:T(8,128)(2,1)}), bf16[8,16,1024]{2,1,0:T(8,128)(2,1)S(1)}, u32[]{:S(2)}, u32[]{:S(2)}) %all-to-all-start) | async-done | bytes 262176 | tf_op jit(solution)/shard_map/all_to_all | solution.py:121
  144.7 0.1 copy.45
  144.8 0.1 reshape.354
  145.0 0.3 convolution_convert_fusion.1
  145.3 1.2 copy.46
  146.5 3.7 %all-to-all-start.1 = ((bf16[8,4,8192]{2,1,0:T(4,128)(2,1)}), bf16[8,4,8192]{2,1,0:T(4,128)(2,1)S(1)}, u32[]{:S(2)}, u32[]{:S(2)}) async-start(bf16[8,4,8192]{2,1,0:T(4,128)(2,1)} %copy.46), calls=%async_computation.1 | async-start | bytes 1048576 | tf_op jit(solution)/shard_map/all_to_all | solution.py:129
  150.2 0.2 reduce-window_clone.1
  150.3 0.1 select_reduce_fusion
  150.4 25.3 %all-to-all-done.1 = bf16[8,4,8192]{2,1,0:T(4,128)(2,1)S(1)} async-done(((bf16[8,4,8192]{2,1,0:T(4,128)(2,1)}), bf16[8,4,8192]{2,1,0:T(4,128)(2,1)S(1)}, u32[]{:S(2)}, u32[]{:S(2)}) %all-to-all-start.1) | async-done | bytes 524320 | tf_op jit(solution)/shard_map/all_to_all | solution.py:129
  175.8 0.1 reshape.349
  175.9 4.8 %fusion.21 = (f32[256]{0:T(256)S(1)}, bf16[256,8192]{1,0:T(8,128)(2,1)}) fusion(bf16[256,8192]{1,0:T(8,128)(2,1)} %param.28, bf16[32,8192]{1,0:T(8,128)(2,1)S(1)} %reshape.349, s32[256]{0:T(256)S(1)} %copy-done.6, pred[256]{0:T(512)(128)(4,1)S(1)} %broadcast_compare_fusion), kind=kOutput, calls=%fused_computation.30 | convolution fusion | flops 144711424 | bytes 8915200 | tf_op jit(solution)/shard_map/dot_general | solution.py:134
  180.7 44.7 %all-gather.9.cloned.1.call-done = bf16[8192,768]{1,0:T(8,128)(2,1)} async-done(((bf16[256,768]{1,0:T(8,128)(2,1)}), bf16[8192,768]{1,0:T(8,128)(2,1)}) %all-gather.9.cloned.1.call-update) | async-done | bytes 12582928 | tf_op jit(solution)/shard_map/all_gather | solution.py:140
  225.4 9.3 %fusion.28 = bf16[256,768]{1,0:T(8,128)(2,1)S(1)} fusion(bf16[8192,768]{1,0:T(8,128)(2,1)} %all-gather.9.cloned.1.call-done, bf16[256,8192]{1,0:T(8,128)(2,1)} %get-tuple-element.202, f32[8192]{0:T(1024)S(1)} %copy-done.5, f32[256]{0:T(256)S(1)} %add_rsqrt_fusion), kind=kOutput, calls=%fused_computation.38 | convolution fusion | flops 3229810688 | bytes 17204224 | tf_op jit(solution)/shard_map/dot_general | solution.py:138
  234.9 30.8 %while.20 = (s32[]{:T(128)}, bf16[256,256]{1,0:T(8,128)(2,1)S(1)}, bf16[1280,256]{1,0:T(8,128)(2,1)S(1)}, s32[]{:T(128)}, s32[]{:T(128)}, /*index=5*/s32[]{:T(128)}, s32[]{:T(128)}, s32[]{:T(128)}) while((s32[]{:T(128)}, bf16[256,256]{1,0:T(8,128)(2,1)S(1)}, bf16[1280,256]{1,0:T(8,128)(2,1)S(1)}, s32[]{:T(128)}, s32[]{:T(128)}, ...), condition=%wide.region_9.10_spmd, body=%wide.region_8.9_spmd.sunk | while | flops 7 | bytes 1048763 | solution.py:164
  234.9 3.4 %collective-permute-start = (bf16[256,256]{1,0:T(8,128)(2,1)S(1)}, bf16[256,256]{1,0:T(8,128)(2,1)S(1)}, u32[]{:S(2)}, u32[]{:S(2)}) collective-permute-start(bf16[256,256]{1,0:T(8,128)(2,1)S(1)} %get-tuple-element.278), channel_id=1, source_target_pairs={{0,1},{1,2},{2,3},{3,4},{4,5},{5,6},{6,7},{8,9},{9,10},{10,11},{11... | collective-permute-start | bytes 393224 | tf_op jit(solution)/shard_map/while/body/eval_jaxpr/ppermute | solution.py:16
  238.3 3.1 collective-permute-done
  241.5 4.4 %collective-permute-start = (bf16[256,256]{1,0:T(8,128)(2,1)S(1)}, bf16[256,256]{1,0:T(8,128)(2,1)S(1)}, u32[]{:S(2)}, u32[]{:S(2)}) collective-permute-start(bf16[256,256]{1,0:T(8,128)(2,1)S(1)} %get-tuple-element.278), channel_id=1, source_target_pairs={{0,1},{1,2},{2,3},{3,4},{4,5},{5,6},{6,7},{8,9},{9,10},{10,11},{11... | collective-permute-start | bytes 393224 | tf_op jit(solution)/shard_map/while/body/eval_jaxpr/ppermute | solution.py:16
  245.9 2.5 collective-permute-done
  248.4 4.5 %collective-permute-start = (bf16[256,256]{1,0:T(8,128)(2,1)S(1)}, bf16[256,256]{1,0:T(8,128)(2,1)S(1)}, u32[]{:S(2)}, u32[]{:S(2)}) collective-permute-start(bf16[256,256]{1,0:T(8,128)(2,1)S(1)} %get-tuple-element.278), channel_id=1, source_target_pairs={{0,1},{1,2},{2,3},{3,4},{4,5},{5,6},{6,7},{8,9},{9,10},{10,11},{11... | collective-permute-start | bytes 393224 | tf_op jit(solution)/shard_map/while/body/eval_jaxpr/ppermute | solution.py:16
  252.9 4.7 %collective-permute-done = bf16[256,256]{1,0:T(8,128)(2,1)S(1)} collective-permute-done((bf16[256,256]{1,0:T(8,128)(2,1)S(1)}, bf16[256,256]{1,0:T(8,128)(2,1)S(1)}, u32[]{:S(2)}, u32[]{:S(2)}) %collective-permute-start) | collective-permute-done | bytes 131104 | tf_op jit(solution)/shard_map/while/body/eval_jaxpr/ppermute | solution.py:16
  257.7 5.5 %collective-permute-start = (bf16[256,256]{1,0:T(8,128)(2,1)S(1)}, bf16[256,256]{1,0:T(8,128)(2,1)S(1)}, u32[]{:S(2)}, u32[]{:S(2)}) collective-permute-start(bf16[256,256]{1,0:T(8,128)(2,1)S(1)} %get-tuple-element.278), channel_id=1, source_target_pairs={{0,1},{1,2},{2,3},{3,4},{4,5},{5,6},{6,7},{8,9},{9,10},{10,11},{11... | collective-permute-start | bytes 393224 | tf_op jit(solution)/shard_map/while/body/eval_jaxpr/ppermute | solution.py:16
  263.2 2.5 collective-permute-done
  265.7 5.9 %while.21 = (s32[]{:T(128)}, bf16[4,256,128]{1,2,0:T(8,128)(2,1)S(1)}, s32[256]{0:T(256)S(1)}, bf16[4,256,128]{2,1,0:T(8,128)(2,1)S(1)}, bf16[1280,256]{1,0:T(8,...) while((s32[]{:T(128)}, bf16[4,256,128]{1,2,0:T(8,128)(2,1)S(1)}, s32[256]{0:T(256)S(1)}, ...), condition=%wide.region_13.14_spmd.clone, body=%wide.region_10.13_spmd.clone.sunk | while | flops 171115520 | bytes 5002341 | solution.py:179
  265.7 0.5 fusion.84
  266.3 0.3 fusion.85
  266.6 0.4 fusion.86
  267.0 0.1 copy.66
  267.2 0.5 fusion.84
  267.7 0.3 fusion.85
  268.1 0.4 fusion.86
  268.5 0.1 copy.66
  268.7 0.5 fusion.84
  269.2 0.3 fusion.85
  269.5 0.4 fusion.86
  270.0 0.1 copy.66
  270.1 0.5 fusion.84
  270.7 0.3 fusion.85
  271.0 0.4 fusion.86
  271.4 0.1 copy.66
  271.6 49.3 %all-gather.11.cloned.1.call-done = bf16[512,8192]{1,0:T(8,128)(2,1)} async-done(((bf16[512,256]{1,0:T(8,128)(2,1)}), bf16[512,8192]{1,0:T(8,128)(2,1)}) %all-gather.11.cloned.1.call-update) | async-done | bytes 8388624 | tf_op jit(solution)/shard_map/all_gather | solution.py:182
  320.9 9.2 %fusion.19 = bf16[256,8192]{1,0:T(8,128)(2,1)} fusion(bf16[256,512]{0,1:T(8,128)(2,1)S(1)} %bitcast.73, bf16[512,8192]{1,0:T(8,128)(2,1)} %all-gather.11.cloned.1.call-done, bf16[256,8192]{1,0:T(8,128)(2,1)} %get-tuple-element.202), kind=kOutput, calls=%fused_computation.26 | convolution fusion | flops 2153775104 | bytes 17039360 | tf_op jit(solution)/shard_map/dot_general | solution.py:180
  (57 shorter events, 0.6 us)
Async XLA Ops:
  6.5 19.4 %copy-start = (bf16[1280,1280]{1,0:T(8,128)(2,1)S(1)}, bf16[1280,1280]{1,0:T(8,128)(2,1)}, u32[]{:S(2)}) copy-start(bf16[1280,1280]{1,0:T(8,128)(2,1)} %param.23) | copy-start | bytes 9830404
  6.5 66.8 %all-gather.5.cloned.1.call-start = ((), (), s32[]{:S(2)}) async-start(), calls=%async_computation.2 | async-start | bytes 1474560 | tf_op jit(solution)/shard_map/all_gather | solution.py:106
  7.8 12.6 %copy-start.4 = (s32[1,64]{1,0:T(1,128)S(1)}, s32[1,64]{1,0:T(1,128)}, u32[]{:S(2)}) copy-start(s32[1,64]{1,0:T(1,128)} %param.20) | copy-start | bytes 772
  13.6 12.4 %copy-start.2 = (bf16[64,1280]{1,0:T(8,128)(2,1)S(1)}, bf16[64,1280]{1,0:T(8,128)(2,1)}, u32[]{:S(2)}) copy-start(bf16[64,1280]{1,0:T(8,128)(2,1)} %param.19) | copy-start | bytes 491524
  21.8 5.9 %copy-start.3 = (f32[1280]{0:T(1024)S(1)}, f32[1280]{0:T(1024)}, u32[]{:S(2)}) copy-start(f32[1280]{0:T(1024)} %param.24) | copy-start | bytes 15364
  28.6 92.0 %all-gather.7.cloned.1.call-start = ((), (), s32[]{:S(2)}) async-start(), calls=%async_computation.3 | async-start | bytes 1474560 | tf_op jit(solution)/shard_map/all_gather | solution.py:113
  79.1 146.3 %all-gather.9.cloned.1.call-start = ((), (), s32[]{:S(2)}) async-start(), calls=%async_computation.4 | async-start | bytes 12976128 | tf_op jit(solution)/shard_map/all_gather | solution.py:140
  79.8 241.0 %all-gather.11.cloned.1.call-start = ((), (), s32[]{:S(2)}) async-start(), calls=%async_computation.5 | async-start | bytes 8650752 | tf_op jit(solution)/shard_map/all_gather | solution.py:182
  80.4 50.4 %copy-start.7 = (s32[16]{0:T(128)S(1)}, s32[16]{0:T(128)}, u32[]{:S(2)}) copy-start(s32[16]{0:T(128)} %param.27) | copy-start | bytes 196
  127.3 22.9 %copy-start.8 = (s32[1,4]{1,0:T(1,128)S(1)}, s32[1,4]{1,0:T(1,128)}, u32[]{:S(2)}) copy-start(s32[1,4]{1,0:T(1,128)} %param.30) | copy-start | bytes 52
  127.3 23.2 %copy-start.6 = (s32[256]{0:T(256)S(1)}, s32[256]{0:T(256)}, u32[]{:S(2)}) copy-start(s32[256]{0:T(256)} %param.29) | copy-start | bytes 3076
  127.3 17.4 %all-to-all-start = ((bf16[8,16,1024]{2,1,0:T(8,128)(2,1)}), bf16[8,16,1024]{2,1,0:T(8,128)(2,1)S(1)}, u32[]{:S(2)}, u32[]{:S(2)}) async-start(bf16[8,16,1024]{2,1,0:T(8,128)(2,1)} %bitcast.3), calls=%async_computation | async-start | bytes 524288 | tf_op jit(solution)/shard_map/all_to_all | solution.py:121
  146.5 29.3 %all-to-all-start.1 = ((bf16[8,4,8192]{2,1,0:T(4,128)(2,1)}), bf16[8,4,8192]{2,1,0:T(4,128)(2,1)S(1)}, u32[]{:S(2)}, u32[]{:S(2)}) async-start(bf16[8,4,8192]{2,1,0:T(4,128)(2,1)} %copy.46), calls=%async_computation.1 | async-start | bytes 1048576 | tf_op jit(solution)/shard_map/all_to_all | solution.py:129
  175.9 49.5 %copy-start.5 = (f32[8192]{0:T(1024)S(1)}, f32[8192]{0:T(1024)}, u32[]{:S(2)}) copy-start(f32[8192]{0:T(1024)} %param.31) | copy-start | bytes 98308
  234.9 6.5 %collective-permute-start = (bf16[256,256]{1,0:T(8,128)(2,1)S(1)}, bf16[256,256]{1,0:T(8,128)(2,1)S(1)}, u32[]{:S(2)}, u32[]{:S(2)}) collective-permute-start(bf16[256,256]{1,0:T(8,128)(2,1)S(1)} %get-tuple-element.278), channel_id=1, source_target_pairs={{0,1},{1,2},{2,3},{3,4},{4,5},{5,6},{6,7},{8,9},{9,10},{10,11},{11... | collective-permute-start | bytes 393224 | tf_op jit(solution)/shard_map/while/body/eval_jaxpr/ppermute | solution.py:16
  241.5 6.9 %collective-permute-start = (bf16[256,256]{1,0:T(8,128)(2,1)S(1)}, bf16[256,256]{1,0:T(8,128)(2,1)S(1)}, u32[]{:S(2)}, u32[]{:S(2)}) collective-permute-start(bf16[256,256]{1,0:T(8,128)(2,1)S(1)} %get-tuple-element.278), channel_id=1, source_target_pairs={{0,1},{1,2},{2,3},{3,4},{4,5},{5,6},{6,7},{8,9},{9,10},{10,11},{11... | collective-permute-start | bytes 393224 | tf_op jit(solution)/shard_map/while/body/eval_jaxpr/ppermute | solution.py:16
  248.4 9.2 %collective-permute-start = (bf16[256,256]{1,0:T(8,128)(2,1)S(1)}, bf16[256,256]{1,0:T(8,128)(2,1)S(1)}, u32[]{:S(2)}, u32[]{:S(2)}) collective-permute-start(bf16[256,256]{1,0:T(8,128)(2,1)S(1)} %get-tuple-element.278), channel_id=1, source_target_pairs={{0,1},{1,2},{2,3},{3,4},{4,5},{5,6},{6,7},{8,9},{9,10},{10,11},{11... | collective-permute-start | bytes 393224 | tf_op jit(solution)/shard_map/while/body/eval_jaxpr/ppermute | solution.py:16
  257.7 8.0 %collective-permute-start = (bf16[256,256]{1,0:T(8,128)(2,1)S(1)}, bf16[256,256]{1,0:T(8,128)(2,1)S(1)}, u32[]{:S(2)}, u32[]{:S(2)}) collective-permute-start(bf16[256,256]{1,0:T(8,128)(2,1)S(1)} %get-tuple-element.278), channel_id=1, source_target_pairs={{0,1},{1,2},{2,3},{3,4},{4,5},{5,6},{6,7},{8,9},{9,10},{10,11},{11... | collective-permute-start | bytes 393224 | tf_op jit(solution)/shard_map/while/body/eval_jaxpr/ppermute | solution.py:16
  320.9 9.2 %copy-start.1 = (bf16[1280,1280]{1,0:T(8,128)(2,1)S(1)}, bf16[1280,1280]{1,0:T(8,128)(2,1)}, u32[]{:S(2)}) copy-start(bf16[1280,1280]{1,0:T(8,128)(2,1)} %param.23) | copy-start | bytes 9830404
Sparse Core Ops, SparseCore 0:
  28.7 44.5 all-gather.4
  79.2 41.3 all-gather.6
  123.6 101.8 all-gather.8
  228.2 92.6 all-gather.10
where the time goes:
time: 337 us
  waiting for transfers between devices  232 us (69%)
  matrix products  49.9 us (15%)
  starting transfers between devices  25.1 us (7%)
  between operations  13.4 us (4%)
  local copies, waits for them, and re-layouts  12.6 us (4%)
  other arithmetic  3.41 us (1%)
    all_gather x1, waiting for transfers between devices, on_device(): lax.all_gather(attn_out, ('grp', 'seq'), axis=1, tiled=True)  49.3 us
    all_gather x1, waiting for transfers between devices, on_device(): lax.all_gather(attn_qkv, ('grp', 'seq'), axis=0, tiled=True)  44.7 us
    all_gather x1, waiting for transfers between devices, on_device(): lax.all_gather(merge_input, 'seq', axis=0, tiled=True)  44.6 us
    all_gather x1, waiting for transfers between devices, on_device(): lax.all_gather(hidden_part, 'seq', axis=1, tiled=True)  40.2 us
    all_to_all x1, waiting for transfers between devices, on_device(): lax.all_to_all(outgoing, 'seq', split_axis=0, concat_axis=0, tiled=True)  25.3 us
    ppermute x4, starting transfers between devices, from_behind(): lax.ppermute(value, axis, [(source, source + steps) for source in range(f...  17.7 us
    all_to_all x1, waiting for transfers between devices, on_device(): lax.all_to_all(column_part, 'seq', split_axis=0, concat_axis=1, tiled=True)  13.7 us
    ppermute x4, waiting for transfers between devices, from_behind(): lax.ppermute(value, axis, [(source, source + steps) for source in range(f...  12.8 us
  transfers between devices with their start and end apart: 10, of which 10 were waited for; matrix products, arithmetic and copies ran while one was open for 9% of the time, Pallas kernels for 0%

commit v1 on v0

v1 whole, which is shorter than its diff:
```python
import functools

import jax
import jax.numpy as jnp
from jax import lax
from jax.experimental import pallas as pl
from jax.experimental.pallas import tpu as pltpu
from jax.sharding import PartitionSpec as P

VHEADS = 16
WIN = 64
LANES = 128
EPSILON = 1e-06
MESH = pl.DeviceIdType.MESH


def rms_scale(inputs, gain):
    mean_square = jnp.mean(inputs * inputs, axis=-1, keepdims=True)
    return inputs * lax.rsqrt(mean_square + EPSILON) * gain


def slot_numbers(targets):
    row_count = targets.shape[-1]
    order = jnp.arange(row_count, dtype=jnp.int32)
    same = targets[..., :, None] == targets[..., None, :]
    earlier = order[None, :] < order[:, None]
    return jnp.sum(same & earlier, axis=-1)


def greet(n_seq, pairs):
    grp, seq = lax.axis_index("grp"), lax.axis_index("seq")
    barrier = pltpu.get_barrier_semaphore()
    for k in range(1, n_seq):
        pl.semaphore_signal(
            barrier, inc=1, device_id=(grp, lax.rem(seq + k, n_seq)), device_id_type=MESH
        )
    for other in pairs:
        pl.semaphore_signal(barrier, inc=1, device_id=(other, seq), device_id_type=MESH)
    pl.semaphore_wait(barrier, n_seq - 1 + len(pairs))


def flip(index, bit):
    return index + bit - 2 * bit * lax.rem(index // bit, 2)


class Relay:
    def __init__(self, n_seq, shard, full, local_sem, recv_sem, send_sem):
        self.n_seq, self.shard, self.full = n_seq, shard, full
        self.local_sem, self.recv_sem, self.send_sem = local_sem, recv_sem, send_sem
        self.line = n_seq // 2
        self.grp, self.seq = lax.axis_index("grp"), lax.axis_index("seq")
        self.core = lax.rem(self.grp, 2)
        self.place, self.side = self.seq // 2, lax.rem(self.seq, 2)
        far = flip(self.grp, 2)
        self.far = far
        across = flip(self.seq, 1)
        first = self.core == 0
        self.a_dev = (jnp.where(first, far, self.grp), jnp.where(first, self.seq, across))
        self.b_dev = (jnp.where(first, self.grp, far), jnp.where(first, across, self.seq))
        self.ab_dev = (far, across)
        self.core_dev = (flip(self.grp, 1), self.seq)

    def slot(self, base, place):
        return base[0] * self.n_seq + 2 * place + lax.rem(base[1], 2)

    def copy(self, slot, way, device, own=False):
        return pltpu.make_async_remote_copy(
            src_ref=self.shard if own else self.full.at[slot],
            dst_ref=self.full.at[slot],
            send_sem=self.send_sem.at[way, slot],
            recv_sem=self.recv_sem.at[slot],
            device_id=device,
            device_id_type=MESH,
        )

    def up(self):
        return (self.grp, jnp.minimum(self.seq + 2, self.n_seq - 2 + self.side))

    def down(self):
        return (self.grp, jnp.maximum(self.seq - 2, self.side))

    def me(self):
        return (self.grp, self.seq)

    def begin(self):
        slot = self.slot(self.me(), self.place)
        pltpu.make_async_copy(self.shard, self.full.at[slot], self.local_sem).start()

        @pl.when(self.place + 1 < self.line)
        def _():
            self.copy(slot, 0, self.up(), True).start()

        @pl.when(self.place > 0)
        def _():
            self.copy(slot, 1, self.down(), True).start()

        self.copy(slot, 2, self.a_dev, True).start()
        self.copy(slot, 3, self.b_dev, True).start()
        self.copy(slot, 4, self.core_dev, True).start()

    def spots(self, distance):
        low, high = self.place - distance, self.place + distance
        if distance == 0:
            return [(self.place, None, None)]
        return [(low, low >= 0, True), (high, high < self.line, False)]

    def visit(self, base, distance, ways, finish=False):
        for place, there, upward in self.spots(distance):

            def act(place=place, upward=upward):
                slot = self.slot(base, place)
                own_core = base is not None
                if not finish:
                    self.copy(slot, 4, self.core_dev).wait_recv()
                for way, device in ways:
                    move = self.copy(slot, way, device)
                    move.wait_send() if finish else move.start()
                if upward is True and "z" in self.mode:

                    @pl.when(self.place + 1 < self.line)
                    def _():
                        move = self.copy(slot, 0, self.up())
                        move.wait_send() if finish else move.start()

                if upward is False and "z" in self.mode:

                    @pl.when(self.place > 0)
                    def _():
                        move = self.copy(slot, 1, self.down())
                        move.wait_send() if finish else move.start()

            if there is None:
                act()
            else:
                pl.when(there)(act)

    def own_line(self, distance, finish=False):
        self.mode = "z"
        self.visit(
            self.me(), distance,
            [(2, self.a_dev), (3, self.b_dev), (4, self.core_dev)], finish,
        )

    def a_line(self, distance, finish=False):
        self.mode = ""
        self.visit(self.a_dev, distance, [(3, self.b_dev), (4, self.core_dev)], finish)

    def b_lines(self, distance, finish=False):
        self.mode = ""
        self.visit(self.b_dev, distance, [(4, self.core_dev)], finish)
        self.visit(self.ab_dev, distance, [(4, self.core_dev)], finish)

    def step(self, distance):
        if 0 < distance < self.line:
            self.own_line(distance)
        if 0 <= distance - 1 < self.line:
            self.a_line(distance - 1)
        if 0 <= distance - 2 < self.line:
            self.b_lines(distance - 2)

    def steps(self):
        return self.line + 2

    def end(self):
        slot = self.slot(self.me(), self.place)
        pltpu.make_async_copy(self.shard, self.full.at[slot], self.local_sem).wait()

        @pl.when(self.place + 1 < self.line)
        def _():
            self.copy(slot, 0, self.up(), True).wait_send()

        @pl.when(self.place > 0)
        def _():
            self.copy(slot, 1, self.down(), True).wait_send()

        self.copy(slot, 2, self.a_dev, True).wait_send()
        self.copy(slot, 3, self.b_dev, True).wait_send()
        self.copy(slot, 4, self.core_dev, True).wait_send()
        for distance in range(self.line):
            if distance:
                self.own_line(distance, True)
            self.a_line(distance, True)
            self.b_lines(distance, True)
        partner = self.core_dev[0]
        for place in range(self.line):
            for base in (
                (partner, self.seq), (partner, flip(self.seq, 1)),
                (flip(partner, 2), self.seq), (flip(partner, 2), flip(self.seq, 1)),
            ):
                slot = self.slot(base, place)
                self.copy(slot, 4, self.core_dev).wait_recv()


def relay_scratch(n_dev):
    return [
        pltpu.SemaphoreType.DMA,
        pltpu.SemaphoreType.DMA((n_dev,)),
        pltpu.SemaphoreType.DMA((5, n_dev)),
    ]


def swap(n_seq, send_of, land_of, send_sem, recv_sem):
    grp, seq = lax.axis_index("grp"), lax.axis_index("seq")
    moves = []
    for k in range(1, n_seq):
        to = lax.rem(seq + k, n_seq)
        moves.append(
            pltpu.make_async_remote_copy(
                src_ref=send_of(to),
                dst_ref=land_of(seq),
                send_sem=send_sem.at[k],
                recv_sem=recv_sem.at[k],
                device_id=(grp, to),
                device_id_type=MESH,
            )
        )
    for move in moves:
        move.start()
    return moves


def vision_kernel(
    n_seq, slots,
    patches, piece_col, piece_row, vit_gain, vit_qkv, vit_out, merge_gain, merge_up, merge_down,
    code, want, row_base, attn_qkv,
    table, qkv_all,
    up_v, down_v, normed_s, gathered, hidden, stage, landed,
    load_sem, send1, recv1, send2, recv2, send3, recv3, *relay_sems,
):
    seq = lax.axis_index("seq")
    grp = lax.axis_index("grp")
    up_copy = pltpu.make_async_copy(merge_up, up_v, load_sem.at[0])
    down_copy = pltpu.make_async_copy(merge_down, down_v, load_sem.at[1])
    up_copy.start()
    down_copy.start()
    greet(n_seq, (flip(grp, 1), flip(grp, 2)))
    relay = Relay(n_seq, attn_qkv, qkv_all, *relay_sems)
    relay.begin()

    rows, features = patches.shape
    head_dim = features // VHEADS
    residual = patches[...].astype(jnp.float32)
    normed = rms_scale(residual, vit_gain[...]).astype(jnp.bfloat16)
    projected = jnp.dot(normed, vit_qkv[...], preferred_element_type=jnp.float32)
    q = projected[:, :features].astype(jnp.bfloat16).astype(jnp.float32)
    keys = projected[:, features : 2 * features].astype(jnp.bfloat16)
    values = projected[:, 2 * features :].astype(jnp.bfloat16)
    lane = lax.broadcasted_iota(jnp.int32, (rows, features), 1)
    inside = [(lane >= h * head_dim) & (lane < (h + 1) * head_dim) for h in range(VHEADS)]
    stacked = jnp.concatenate(
        [jnp.where(inside[h], q, 0.0).astype(jnp.bfloat16) for h in range(VHEADS)], axis=0
    )
    scores = lax.dot_general(
        stacked, keys, (((1,), (1,)), ((), ())), preferred_element_type=jnp.float32
    ) * head_dim ** (-0.5)
    scores = scores.reshape(VHEADS, rows, rows)
    allowed = piece_col[...] == piece_row[...]
    scores = jnp.where(allowed[None], scores, -1e30)
    weights = jnp.exp(scores - jnp.max(scores, axis=-1, keepdims=True))
    totals = jnp.sum(weights, axis=-1, keepdims=True)
    mixed = jnp.dot(
        weights.reshape(VHEADS * rows, rows).astype(jnp.bfloat16), values,
        preferred_element_type=jnp.float32,
    )
    top = jnp.zeros((rows, features), jnp.float32)
    low = jnp.ones((rows, features), jnp.float32)
    for h in range(VHEADS):
        top = jnp.where(inside[h], mixed[h * rows : (h + 1) * rows], top)
        low = jnp.where(inside[h], totals[h], low)
    mixture = (top / low).astype(jnp.bfloat16)
    residual = residual + jnp.dot(mixture, vit_out[...], preferred_element_type=jnp.float32)
    merged_in = rms_scale(residual, merge_gain[...])
    own = rows // 4
    chunks = features // LANES
    for j in range(chunks):
        normed_s[j] = merged_in[:, j * LANES : (j + 1) * LANES]
    for part in range(4):
        for j in range(chunks):
            start = part * features + j * LANES
            gathered[seq, :, start : start + LANES] = normed_s[
                j, pl.ds(part, own, stride=4), :
            ].astype(jnp.bfloat16)
    gathered[seq, :, 4 * features :] = code[...]
    moves1 = swap(n_seq, lambda to: gathered.at[seq], lambda me: gathered.at[me], send1, recv1)
    up_copy.wait()
    for move in moves1:
        move.wait_recv()
    all_rows = n_seq * own
    entry = gathered[:, :, : 4 * features].reshape(all_rows, 4 * features)
    pre = jnp.dot(entry, up_v[...], preferred_element_type=jnp.float32)
    hidden[seq] = (0.5 * pre * (1.0 + lax.erf(pre * 0.5**0.5))).astype(jnp.bfloat16)
    moves2 = swap(n_seq, lambda to: hidden.at[seq], lambda me: hidden.at[me], send2, recv2)
    down_copy.wait()
    part_width = hidden.shape[2]

    def term(source):
        start = pl.multiple_of(source * part_width, 32)
        return jnp.dot(
            hidden[source], down_v[pl.ds(start, part_width), :], preferred_element_type=jnp.float32
        )

    codes = gathered[:, :, 4 * features :].reshape(all_rows, LANES).astype(jnp.float32)[:, :1]
    select = jnp.where(codes + row_base[...] == want[...], 1.0, 0.0)
    select = jnp.transpose(select).astype(jnp.bfloat16)
    total = term(seq)
    for k in range(1, n_seq):
        moves2[k - 1].wait_recv()
        total = total + term(lax.rem(seq - k + n_seq, n_seq))
    outgoing = jnp.dot(
        select, total.astype(jnp.bfloat16), preferred_element_type=jnp.float32
    ).astype(jnp.bfloat16)
    stage[...] = outgoing.reshape(stage.shape)
    landed[seq] = stage[seq]
    moves3 = swap(n_seq, lambda to: stage.at[to], lambda me: landed.at[me], send3, recv3)
    for distance in range(relay.steps()):
        relay.step(distance)
    for move in moves3:
        move.wait_recv()
    width = landed.shape[2]
    for source in range(n_seq):
        table[:, source * width : (source + 1) * width] = landed[source]
    for moves in (moves1, moves2, moves3):
        for move in moves:
            move.wait_send()
    relay.end()


def attend_kernel(
    n_seq, reach, heads,
    queries, own_kv, positions, starts, attn_out,
    attended, out_all,
    kv, load_sem, send_sem, recv_sem, *relay_sems,
):
    grp, seq = lax.axis_index("grp"), lax.axis_index("seq")
    rows, width = own_kv.shape
    head_dim = width // 2
    greet(n_seq, (flip(grp, 1), flip(grp, 2)))
    moves = []
    for k in range(1, reach + 1):
        moves.append(
            pltpu.make_async_remote_copy(
                src_ref=own_kv,
                dst_ref=kv.at[reach - k],
                send_sem=send_sem.at[k],
                recv_sem=recv_sem.at[k],
                device_id=(grp, lax.rem(seq + k, n_seq)),
                device_id_type=MESH,
            )
        )
    for move in moves:
        move.start()
    relay = Relay(n_seq, attn_out, out_all, *relay_sems)
    relay.begin()
    kv[reach] = own_kv[...]
    for move in moves:
        move.wait_recv()
    span = (reach + 1) * rows
    everything = kv[...].reshape(span, width)
    keys, values = everything[:, :head_dim], everything[:, head_dim:]
    key_pos = (seq - reach) * rows + lax.broadcasted_iota(jnp.int32, (rows, span), 1)
    allowed = (key_pos >= starts[...]) & (key_pos <= positions[...])
    for distance in range(relay.steps()):
        relay.step(distance)
        for h in range(heads) if distance == 1 else ():
            scores = lax.dot_general(
                queries[:, h * head_dim : (h + 1) * head_dim], keys,
                (((1,), (1,)), ((), ())), preferred_element_type=jnp.float32,
            ) * head_dim ** (-0.5)
            scores = jnp.where(allowed, scores, -1e30)
            weights = jnp.exp(scores - jnp.max(scores, axis=-1, keepdims=True))
            totals = jnp.sum(weights, axis=-1, keepdims=True)
            mixed = jnp.dot(
                weights.astype(jnp.bfloat16), values, preferred_element_type=jnp.float32
            )
            attended[:, h * head_dim : (h + 1) * head_dim] = (mixed / totals).astype(jnp.bfloat16)
    for move in moves:
        move.wait_send()
    relay.end()


def out_kernel(attended, weight, layer_in, result):
    width = weight.shape[2]
    for i in range(weight.shape[0]):
        columns = slice(i * width, (i + 1) * width)
        update = jnp.dot(attended[...], weight[i], preferred_element_type=jnp.float32)
        result[:, columns] = (layer_in[:, columns].astype(jnp.float32) + update).astype(jnp.bfloat16)


VMEM = pl.BlockSpec(memory_space=pltpu.VMEM)
ANY = pl.BlockSpec(memory_space=pl.ANY)


def on_device(
    patches, piece_ids, vit_gain, vit_qkv, vit_out, merge_gain, merge_up, merge_down, dest,
    tokens, image_index, doc_lengths, attn_gain, attn_qkv, attn_out,
):
    rows, features = patches.shape
    n_seq, n_grp = lax.axis_size("seq"), lax.axis_size("grp")
    n_dev = n_seq * n_grp
    seq_index = lax.axis_index("seq")
    own = rows // 4
    all_rows = n_seq * own
    capacity = own // (n_seq // 2)
    slots = n_seq * capacity
    bf16, f32 = jnp.bfloat16, jnp.float32

    windows = jnp.arange(rows, dtype=jnp.int32) // WIN
    pieces = piece_ids.reshape(-1) + windows * WIN
    code = dest * capacity + slot_numbers(dest).astype(jnp.int32)
    code = jnp.broadcast_to(code[:, None], (own, LANES)).astype(bf16)
    column = jnp.arange(n_seq * slots, dtype=jnp.int32)
    target, place = column // slots, column % slots
    want = (place // capacity) * (n_seq * capacity) + target * capacity + place % capacity
    row_base = (jnp.arange(all_rows, dtype=jnp.int32) // own) * (n_seq * capacity)

    up_width, down_width = merge_up.shape[1], merge_down.shape[1]
    table, qkv_all = pl.pallas_call(
        functools.partial(vision_kernel, n_seq, slots),
        out_shape=(
            jax.ShapeDtypeStruct((slots, n_seq * down_width), bf16),
            jax.ShapeDtypeStruct((n_dev,) + attn_qkv.shape, bf16),
        ),
        in_specs=[VMEM] * 7 + [ANY] * 2 + [VMEM] * 3 + [ANY],
        out_specs=(VMEM, ANY),
        scratch_shapes=[
            pltpu.VMEM(merge_up.shape, bf16),
            pltpu.VMEM(merge_down.shape, bf16),
            pltpu.VMEM((features // LANES, rows, LANES), f32),
            pltpu.VMEM((n_seq, own, 4 * features + LANES), bf16),
            pltpu.VMEM((n_seq, all_rows, up_width), bf16),
            pltpu.VMEM((n_seq, slots, down_width), bf16),
            pltpu.VMEM((n_seq, slots, down_width), bf16),
            pltpu.SemaphoreType.DMA((2,)),
        ] + [pltpu.SemaphoreType.DMA((n_seq,))] * 6 + relay_scratch(n_dev),
        compiler_params=pltpu.CompilerParams(
            collective_id=0, has_side_effects=True, vmem_limit_bytes=66000000
        ),
    )(
        patches, pieces[:, None], pieces[None, :], vit_gain[None], vit_qkv, vit_out,
        merge_gain[None], merge_up, merge_down, code, want.astype(f32)[None],
        row_base.astype(f32)[:, None], attn_qkv,
    )

    slot_all = jnp.arange(slots, dtype=jnp.int32)
    picker = (image_index[:, None] == slot_all[None, :]).astype(bf16)
    pictured = jnp.dot(picker, table, preferred_element_type=f32).astype(bf16)
    layer_in = jnp.where((image_index < slots)[:, None], pictured, tokens)
    tok_rows = tokens.shape[0]
    normed = rms_scale(layer_in.astype(f32), attn_gain).astype(bf16)
    projected = jnp.dot(
        normed, qkv_all.reshape(-1, attn_qkv.shape[1]), preferred_element_type=f32
    ).astype(bf16)
    query_width = attn_out.shape[0]
    queries = projected[:, :query_width]
    key_value = projected[:, query_width:]
    head_dim = key_value.shape[1] // 2
    head_count = query_width // head_dim
    positions = seq_index * tok_rows + jnp.arange(tok_rows, dtype=jnp.int32)
    lengths = doc_lengths[0]
    starts = jnp.cumsum(lengths) - lengths
    doc_start = jnp.max(
        jnp.where(starts[None, :] <= positions[:, None], starts[None, :], 0), axis=1
    )
    reach = n_seq // 2
    attended, out_all = pl.pallas_call(
        functools.partial(attend_kernel, n_seq, reach, head_count),
        out_shape=(
            jax.ShapeDtypeStruct((tok_rows, query_width), bf16),
            jax.ShapeDtypeStruct((n_dev,) + attn_out.shape, bf16),
        ),
        in_specs=[VMEM] * 4 + [ANY],
        out_specs=(VMEM, ANY),
        scratch_shapes=[
            pltpu.VMEM((reach + 1, tok_rows, 2 * head_dim), bf16),
            pltpu.SemaphoreType.DMA((2,)),
            pltpu.SemaphoreType.DMA((reach + 1,)),
            pltpu.SemaphoreType.DMA((reach + 1,)),
        ] + relay_scratch(n_dev),
        compiler_params=pltpu.CompilerParams(
            collective_id=1, has_side_effects=True, vmem_limit_bytes=60000000
        ),
    )(queries, key_value, positions[:, None], doc_start[:, None], attn_out)

    step = n_dev // 8
    wide = step * attn_out.shape[1]
    return pl.pallas_call(
        out_kernel,
        grid=(n_dev // step,),
        out_shape=jax.ShapeDtypeStruct(tokens.shape, bf16),
        in_specs=[
            pl.BlockSpec((tok_rows, query_width), lambda i: (0, 0)),
            pl.BlockSpec((step,) + attn_out.shape, lambda i: (i, 0, 0)),
            pl.BlockSpec((tok_rows, wide), lambda i: (0, i)),
        ],
        out_specs=pl.BlockSpec((tok_rows, wide), lambda i: (0, i)),
    )(attended, out_all, layer_in)


def solution(mesh):
    placed = (
        P(("grp", "seq"), None),
        P(("grp", "seq"), None),
        P(),
        P(),
        P(),
        P(),
        P(None, "seq"),
        P(None, "seq"),
        P(("grp", "seq")),
        P(("grp", "seq"), None),
        P(("grp", "seq")),
        P("grp", None),
        P(),
        P(("grp", "seq"), None),
        P(None, ("grp", "seq")),
    )
    return jax.shard_map(
        on_device, mesh=mesh, in_specs=placed, out_specs=P(("grp", "seq"), None), check_vma=False
    )
```

time: 337 us -> 232 us (0.69)
  waiting for transfers between devices: 232 us -> 0 us
  Pallas kernels: 0 us -> 207 us
  matrix products: 49.9 us -> 12 us
  starting transfers between devices: 25.1 us -> 0 us
  between operations: 13.4 us -> 0.1 us
  local copies, waits for them, and re-layouts: 12.6 us -> 6.19 us
    pallas_call x0 -> x3, Pallas kernels: none -> 207 us  [the longest x1 129 us: on_device(): pl.pallas_call(functools.partial(vision_kernel, n_seq, slots), out_shape=...]
    all_gather x4 -> x0, waiting for transfers between devices: 179 us -> none  [the longest x1 49.3 us: on_device(): lax.all_gather(attn_out, ('grp', 'seq'), axis=1, tiled=True)]
    all_to_all x2 -> x0, waiting for transfers between devices: 39 us -> none  [the longest x1 25.3 us: on_device(): lax.all_to_all(outgoing, 'seq', split_axis=0, concat_axis=0, tiled=True)]
    dot_general x18 -> x2, matrix products: 49.9 us -> 12 us  [the longest x1 8.13 us: on_device(): jnp.dot(normed, qkv_all.reshape(-1, attn_qkv.shape[1]), preferred_element...]
    ppermute x4 -> x0, starting transfers between devices: 17.7 us -> none  [from_behind(): lax.ppermute(value, axis, [(source, source + steps) for source in range(f...]
    ppermute x4 -> x0, waiting for transfers between devices: 12.8 us -> none  [from_behind(): lax.ppermute(value, axis, [(source, source + steps) for source in range(f...]
    all_to_all x2 -> x0, starting transfers between devices: 7.22 us -> none  [the longest x1 3.67 us: on_device(): lax.all_to_all(outgoing, 'seq', split_axis=0, concat_axis=0, tiled=True)]
    reshape x5 -> x1, local copies, waits for them, and re-layouts: 6.88 us -> 0.74 us  [on_device(): pieces = piece_ids.reshape(-1) + windows * WIN]
  transfers between devices with their start and end apart: 10 -> 0, of which waited for: 10 -> 0; matrix products, arithmetic and copies ran while one was open for 9% -> 0% of each run, Pallas kernels for 0% -> 0%
where the time goes in v1:
time: 232 us; the launch traced here: 231 us
  Pallas kernels  207 us (89%)
  matrix products  12 us (5%)
  local copies, waits for them, and re-layouts  6.19 us (3%)
  other arithmetic  5.6 us (2%)
    pallas_call x1, Pallas kernels, on_device(): pl.pallas_call(functools.partial(vision_kernel, n_seq, slots), out_shape=...  129 us
    pallas_call x1, Pallas kernels, on_device(): pl.pallas_call(functools.partial(attend_kernel, n_seq, reach, head_count)...  67.9 us
    pallas_call x1, Pallas kernels, on_device(): pl.pallas_call(out_kernel, grid=(n_dev // step,), out_shape=jax.ShapeDtyp...  10.2 us
    dot_general x1, matrix products, on_device(): jnp.dot(normed, qkv_all.reshape(-1, attn_qkv.shape[1]), preferred_element...  8.13 us

profile of v1, /device:TPU:0, one launch (start us, length us, event | category | flops | bytes accessed | tf_op | source)
XLA Modules:
  0.0 231.1 jit_solution(17516764090494602691)
XLA Ops:
  0.0 0.7 copy.22
  0.7 0.6 fusion.18.piece_col
  1.4 1.2 fusion.28.piece_row
  2.6 1.3 broadcast_in_dim.23.vit_gain
  3.9 1.3 broadcast_in_dim.24.merge_gain
  5.2 0.9 convert_reduce_fusion
  6.1 0.7 add_convert_fusion
  6.8 0.7 broadcast_in_dim.25.code
  7.4 0.6 fusion.26.want
  8.0 0.6 fusion.12.row_base
  8.7 0.0 copy-start.2
  8.7 129.2 %shard_map.145 = (bf16[32,8192]{1,0:T(8,128)(2,1)}, bf16[32,256,768]{2,1,0:T(8,128)(2,1)}) custom-call(bf16[64,1280]{1,0:T(8,128)(2,1)} %patches.1, s32[64,1]{1,0:T(8,128)} %fusion.18.piece_col, s32[1,64]{1,0:T(1,128)} %fusion.28.piece_row, f32[1,1280]{1,0:T(1,128)} %broadcast_in_dim.23.vit_gain, bf16[1280,3840]{1,0:T(8,128)(2,1)} %vit_qkv.1, ...), custom_call_target="tpu_custom_call" | custom-call | tf_op jit(solution)/shard_map/pallas_call | solution.py:417
  137.9 0.0 copy-start.1
  137.9 0.0 copy-done.2
  138.0 3.8 %fusion.1 = (f32[256]{0:T(256)S(1)}, bf16[256,8192]{1,0:T(8,128)(2,1)S(1)}) fusion(bf16[256,8192]{1,0:T(8,128)(2,1)} %param.24, bf16[32,8192]{1,0:T(8,128)(2,1)} %get-tuple-element.9, s32[256]{0:T(256)S(1)} %copy-done.2, pred[256]{0:T(512)(128)(4,1)S(1)} %broadcast_compare_fusion), kind=kOutput, calls=%fused_computation.4 | convolution fusion | flops 144711424 | bytes 8915200 | tf_op jit(solution)/shard_map/dot_general | solution.py:446
  141.8 0.0 copy-start
  141.8 0.0 copy-done.1
  141.8 0.0 copy-start.3
  141.8 8.1 %fusion.8 = bf16[256,768]{1,0:T(8,128)(2,1)S(1)} fusion(bf16[8192,768]{1,0:T(8,128)(2,1)} %bitcast.9, bf16[256,8192]{1,0:T(8,128)(2,1)S(1)} %get-tuple-element.14.layer_in, f32[8192]{0:T(1024)S(1)} %copy-done.1, f32[256]{0:T(256)S(1)} %add_rsqrt_fusion), kind=kOutput, calls=%fused_computation.10 | convolution fusion | flops 3229810688 | bytes 17204224 | tf_op jit(solution)/shard_map/dot_general | solution.py:450
  150.0 0.0 copy-done
  150.0 0.7 slice.8.queries
  150.7 0.7 slice.9.own_kv
  151.4 0.7 iota_add_fusion.positions
  152.0 0.0 copy-done.3
  152.0 0.2 reduce-window_clone.1
  152.2 0.1 select_reduce_fusion
  152.3 0.8 copy.23.starts
  153.1 67.9 %shard_map.146 = (bf16[256,512]{1,0:T(8,128)(2,1)}, bf16[32,512,256]{2,1,0:T(8,128)(2,1)}) custom-call(bf16[256,512]{1,0:T(8,128)(2,1)} %slice.8.queries, bf16[256,256]{1,0:T(8,128)(2,1)} %slice.9.own_kv, s32[256,1]{1,0:T(8,128)} %iota_add_fusion.positions, s32[256,1]{1,0:T(8,128)} %copy.23.starts, bf16[512,256]{1,0:T(8,128)(2,1)} %attn_out.1), custom_call_target="tpu_custom_call" | custom-call | tf_op jit(solution)/shard_map/pallas_call | solution.py:465
  221.0 10.2 %shard_map.147 = bf16[256,8192]{1,0:T(8,128)(2,1)} custom-call(bf16[256,512]{1,0:T(8,128)(2,1)} %get-tuple-element.11.attended, bf16[32,512,256]{2,1,0:T(8,128)(2,1)} %get-tuple-element.12.weight, bf16[256,8192]{1,0:T(8,128)(2,1)} %copy-done), custom_call_target="tpu_custom_call" | custom-call | tf_op jit(solution)/shard_map/pallas_call | solution.py:486
  (4 shorter events, 0.0 us)
Async XLA Ops:
  8.7 129.3 %copy-start.2 = (s32[256]{0:T(256)S(1)}, s32[256]{0:T(256)}, u32[]{:S(2)}) copy-start(s32[256]{0:T(256)} %param.25) | copy-start | bytes 3076
  137.9 3.9 %copy-start.1 = (f32[8192]{0:T(1024)S(1)}, f32[8192]{0:T(1024)}, u32[]{:S(2)}) copy-start(f32[8192]{0:T(1024)} %param.27) | copy-start | bytes 98308
  141.8 8.2 %copy-start = (bf16[256,8192]{1,0:T(8,128)(2,1)}, bf16[256,8192]{1,0:T(8,128)(2,1)S(1)}, u32[]{:S(2)}) copy-start(bf16[256,8192]{1,0:T(8,128)(2,1)S(1)} %get-tuple-element.14.layer_in) | copy-start | bytes 12582916
  141.8 10.2 %copy-start.3 = (s32[1,4]{1,0:T(1,128)S(1)}, s32[1,4]{1,0:T(1,128)}, u32[]{:S(2)}) copy-start(s32[1,4]{1,0:T(1,128)} %param.26) | copy-start | bytes 52

commit v2 on v1

--- a/solution.py
+++ b/solution.py
@@ -282,6 +282,7 @@
             ].astype(jnp.bfloat16)
     gathered[seq, :, 4 * features :] = code[...]
     moves1 = swap(n_seq, lambda to: gathered.at[seq], lambda me: gathered.at[me], send1, recv1)
+    relay.step(1)
     up_copy.wait()
     for move in moves1:
         move.wait_recv()
@@ -290,6 +291,7 @@
     pre = jnp.dot(entry, up_v[...], preferred_element_type=jnp.float32)
     hidden[seq] = (0.5 * pre * (1.0 + lax.erf(pre * 0.5**0.5))).astype(jnp.bfloat16)
     moves2 = swap(n_seq, lambda to: hidden.at[seq], lambda me: hidden.at[me], send2, recv2)
+    relay.step(2)
     down_copy.wait()
     part_width = hidden.shape[2]
 
@@ -312,7 +314,7 @@
     stage[...] = outgoing.reshape(stage.shape)
     landed[seq] = stage[seq]
     moves3 = swap(n_seq, lambda to: stage.at[to], lambda me: landed.at[me], send3, recv3)
-    for distance in range(relay.steps()):
+    for distance in range(3, relay.steps()):
         relay.step(distance)
     for move in moves3:
         move.wait_recv()
@@ -420,7 +422,7 @@
             jax.ShapeDtypeStruct((slots, n_seq * down_width), bf16),
             jax.ShapeDtypeStruct((n_dev,) + attn_qkv.shape, bf16),
         ),
-        in_specs=[VMEM] * 7 + [ANY] * 2 + [VMEM] * 3 + [ANY],
+        in_specs=[VMEM] * 7 + [ANY] * 2 + [VMEM] * 4,
         out_specs=(VMEM, ANY),
         scratch_shapes=[
             pltpu.VMEM(merge_up.shape, bf16),
@@ -468,7 +470,7 @@
             jax.ShapeDtypeStruct((tok_rows, query_width), bf16),
             jax.ShapeDtypeStruct((n_dev,) + attn_out.shape, bf16),
         ),
-        in_specs=[VMEM] * 4 + [ANY],
+        in_specs=[VMEM] * 5,
         out_specs=(VMEM, ANY),
         scratch_shapes=[
             pltpu.VMEM((reach + 1, tok_rows, 2 * head_dim), bf16),

time: 232 us -> 214 us (0.922)
  Pallas kernels: 207 us -> 189 us
    pallas_call x1, Pallas kernels: 129 us -> 114 us  [on_device(): pl.pallas_call(functools.partial(vision_kernel, n_seq, slots), out_shape=...]
where the time goes in v2:
time: 214 us; the launch traced here: 213 us
  Pallas kernels  189 us (88%)
  matrix products  12 us (6%)
  local copies, waits for them, and re-layouts  6.19 us (3%)
  other arithmetic  5.6 us (3%)
    pallas_call x1, Pallas kernels, on_device(): pl.pallas_call(functools.partial(vision_kernel, n_seq, slots), out_shape=...  114 us
    pallas_call x1, Pallas kernels, on_device(): pl.pallas_call(functools.partial(attend_kernel, n_seq, reach, head_count)...  65.6 us
    pallas_call x1, Pallas kernels, on_device(): pl.pallas_call(out_kernel, grid=(n_dev // step,), out_shape=jax.ShapeDtyp...  10.2 us
    dot_general x1, matrix products, on_device(): jnp.dot(normed, qkv_all.reshape(-1, attn_qkv.shape[1]), preferred_element...  8.13 us

profile of v2, /device:TPU:0, one launch (start us, length us, event | category | flops | bytes accessed | tf_op | source)
XLA Modules:
  0.0 213.2 jit_solution(8593538267739588378)
XLA Ops:
  0.0 0.7 copy.22
  0.7 0.6 fusion.18.piece_col
  1.4 1.2 fusion.28.piece_row
  2.6 1.3 broadcast_in_dim.23.vit_gain
  3.9 1.3 broadcast_in_dim.24.merge_gain
  5.2 0.9 convert_reduce_fusion
  6.1 0.7 add_convert_fusion
  6.8 0.7 broadcast_in_dim.25.code
  7.4 0.6 fusion.26.want
  8.0 0.6 fusion.12.row_base
  8.7 0.0 copy-start.2
  8.7 113.6 %shard_map.145 = (bf16[32,8192]{1,0:T(8,128)(2,1)}, bf16[32,256,768]{2,1,0:T(8,128)(2,1)}) custom-call(bf16[64,1280]{1,0:T(8,128)(2,1)} %patches.1, s32[64,1]{1,0:T(8,128)} %fusion.18.piece_col, s32[1,64]{1,0:T(1,128)} %fusion.28.piece_row, f32[1,1280]{1,0:T(1,128)} %broadcast_in_dim.23.vit_gain, bf16[1280,3840]{1,0:T(8,128)(2,1)} %vit_qkv.1, ...), custom_call_target="tpu_custom_call" | custom-call | tf_op jit(solution)/shard_map/pallas_call | solution.py:419
  122.3 0.0 copy-start.1
  122.3 0.0 copy-done.2
  122.3 3.8 %fusion.1 = (f32[256]{0:T(256)S(1)}, bf16[256,8192]{1,0:T(8,128)(2,1)S(1)}) fusion(bf16[256,8192]{1,0:T(8,128)(2,1)} %param.24, bf16[32,8192]{1,0:T(8,128)(2,1)} %get-tuple-element.9, s32[256]{0:T(256)S(1)} %copy-done.2, pred[256]{0:T(512)(128)(4,1)S(1)} %broadcast_compare_fusion), kind=kOutput, calls=%fused_computation.4 | convolution fusion | flops 144711424 | bytes 8915200 | tf_op jit(solution)/shard_map/dot_general | solution.py:448
  126.1 0.0 copy-start
  126.2 0.0 copy-done.1
  126.2 0.0 copy-start.3
  126.2 8.1 %fusion.8 = bf16[256,768]{1,0:T(8,128)(2,1)S(1)} fusion(bf16[8192,768]{1,0:T(8,128)(2,1)} %bitcast.9, bf16[256,8192]{1,0:T(8,128)(2,1)S(1)} %get-tuple-element.14.layer_in, f32[8192]{0:T(1024)S(1)} %copy-done.1, f32[256]{0:T(256)S(1)} %add_rsqrt_fusion), kind=kOutput, calls=%fused_computation.10 | convolution fusion | flops 3229810688 | bytes 17204224 | tf_op jit(solution)/shard_map/dot_general | solution.py:452
  134.3 0.0 copy-done
  134.3 0.7 slice.8.queries
  135.1 0.7 slice.9.own_kv
  135.7 0.7 iota_add_fusion.positions
  136.4 0.0 copy-done.3
  136.4 0.2 reduce-window_clone.1
  136.6 0.1 select_reduce_fusion
  136.6 0.8 copy.23.starts
  137.4 65.6 %shard_map.146 = (bf16[256,512]{1,0:T(8,128)(2,1)}, bf16[32,512,256]{2,1,0:T(8,128)(2,1)}) custom-call(bf16[256,512]{1,0:T(8,128)(2,1)} %slice.8.queries, bf16[256,256]{1,0:T(8,128)(2,1)} %slice.9.own_kv, s32[256,1]{1,0:T(8,128)} %iota_add_fusion.positions, s32[256,1]{1,0:T(8,128)} %copy.23.starts, bf16[512,256]{1,0:T(8,128)(2,1)} %attn_out.1), custom_call_target="tpu_custom_call" | custom-call | tf_op jit(solution)/shard_map/pallas_call | solution.py:467
  203.0 10.2 %shard_map.147 = bf16[256,8192]{1,0:T(8,128)(2,1)} custom-call(bf16[256,512]{1,0:T(8,128)(2,1)} %get-tuple-element.11.attended, bf16[32,512,256]{2,1,0:T(8,128)(2,1)} %get-tuple-element.12.weight, bf16[256,8192]{1,0:T(8,128)(2,1)} %copy-done), custom_call_target="tpu_custom_call" | custom-call | tf_op jit(solution)/shard_map/pallas_call | solution.py:488
  (4 shorter events, 0.0 us)
Async XLA Ops:
  8.7 113.6 %copy-start.2 = (s32[256]{0:T(256)S(1)}, s32[256]{0:T(256)}, u32[]{:S(2)}) copy-start(s32[256]{0:T(256)} %param.25) | copy-start | bytes 3076
  122.3 3.9 %copy-start.1 = (f32[8192]{0:T(1024)S(1)}, f32[8192]{0:T(1024)}, u32[]{:S(2)}) copy-start(f32[8192]{0:T(1024)} %param.27) | copy-start | bytes 98308
  126.1 8.2 %copy-start = (bf16[256,8192]{1,0:T(8,128)(2,1)}, bf16[256,8192]{1,0:T(8,128)(2,1)S(1)}, u32[]{:S(2)}) copy-start(bf16[256,8192]{1,0:T(8,128)(2,1)S(1)} %get-tuple-element.14.layer_in) | copy-start | bytes 12582916
  126.2 10.2 %copy-start.3 = (s32[1,4]{1,0:T(1,128)S(1)}, s32[1,4]{1,0:T(1,128)}, u32[]{:S(2)}) copy-start(s32[1,4]{1,0:T(1,128)} %param.26) | copy-start | bytes 52
